TPU v7x, 32 devices: a whole 2x2x4 slice. The times are simulated.
32 devices in a mesh: span: 4 (over y, x), heads: 8 (over z, core).
Axes of the slice: x: 2, y: 2, z: 4, core: 2. Of those that a mesh axis runs over, the one named last changes fastest.
Arguments:
- latents: bfloat16 [4, 6144, 512], P(None, ('span', 'heads')), may hold values from -6 to 6
- rotary_rows: bfloat16 [4, 6144, 64], P(None, ('span', 'heads')), may hold values from -6 to 6
- latent_gain: float32 [512], replicated, may hold values from 0.25 to 1.75
- key_up: bfloat16 [512, 16, 128], P(None, 'heads'), may hold values from -0.25 to 0.25
- value_up: bfloat16 [512, 16, 128], P(None, 'heads'), may hold values from -0.25 to 0.25
Outputs:
- stored_keys: bfloat16 [4, 6144, 16, 192], P('span', None, 'heads')
- stored_values: bfloat16 [4, 6144, 16, 128], P('span', None, 'heads')
All inputs are finite; a program needn't handle non-finite values.
Results may differ from a plain program's by a relative error of at most 0.001.
Values may be sent and summed in bfloat16 or wider, within the bound.
A program may use at most 128 MiB of HBM per device.

v0:
```python
import jax
import jax.numpy as jnp
from jax import lax
from jax.sharding import PartitionSpec as P


def expand_rows(rows, rotary, key_up, value_up):
    wide_keys = jnp.einsum(
        "btr,rhk->bthk", rows, key_up, preferred_element_type=jnp.float32
    ).astype(jnp.bfloat16)
    shared = jnp.broadcast_to(rotary[:, :, None], wide_keys.shape[:3] + rotary.shape[2:])
    wide_values = jnp.einsum(
        "btr,rhk->bthk", rows, value_up, preferred_element_type=jnp.float32
    ).astype(jnp.bfloat16)
    return (jnp.concatenate([wide_keys, shared], axis=-1), wide_values)


def root_norm(vectors, row_gain):
    return (
        vectors * lax.rsqrt(jnp.mean(vectors * vectors, axis=-1, keepdims=True) + 1e-06) * row_gain
    )


def per_device(latents, rotary_rows, latent_gain, key_up, value_up):
    rows_ready = root_norm(latents.astype(jnp.float32), latent_gain).astype(jnp.bfloat16)
    rows_moved, rotary_moved = (
        lax.all_to_all(rows_ready, "span", split_axis=0, concat_axis=1, tiled=True),
        lax.all_to_all(rotary_rows, "span", split_axis=0, concat_axis=1, tiled=True),
    )
    rows_cut = rows_moved.reshape(
        rows_moved.shape[0], lax.axis_size("span"), -1, rows_moved.shape[2]
    )
    rotary_cut = rotary_moved.reshape(
        rotary_moved.shape[0], lax.axis_size("span"), -1, rotary_moved.shape[2]
    )
    rows_joined, rotary_joined = (
        lax.all_gather(rows_cut, "heads", axis=2, tiled=True),
        lax.all_gather(rotary_cut, "heads", axis=2, tiled=True),
    )
    rows_whole = rows_joined.reshape(rows_joined.shape[0], -1, rows_joined.shape[3])
    rotary_whole = rotary_joined.reshape(rotary_joined.shape[0], -1, rotary_joined.shape[3])
    stored_keys, stored_values = expand_rows(rows_whole, rotary_whole, key_up, value_up)
    return (stored_keys, stored_values)


def solution(mesh):
    in_specs = (
        P(None, ("span", "heads"), None),
        P(None, ("span", "heads"), None),
        P(),
        P(None, "heads", None),
        P(None, "heads", None),
    )
    out_specs = (P("span", None, "heads", None), P("span", None, "heads", None))
    return jax.shard_map(
        per_device, mesh=mesh, in_specs=in_specs, out_specs=out_specs, check_vma=False
    )
```

profile of v0, /device:TPU:0, one launch (start us, length us, event | category | flops | bytes accessed | tf_op | source)
XLA Modules:
  0.0 149.0 jit_solution(12033314378571793330)
XLA Ops:
  7.2 0.0 copy-start
  7.2 0.0 copy-start.2
  7.2 0.0 all-gather.4.cloned.1.call-start
  7.2 1.4 fusion.1
  8.7 1.4 fusion.3
  10.1 16.4 %all_to_all.8 = bf16[4,192,512]{2,1,0:T(8,128)(2,1)} all-to-all(bf16[4,192,512]{2,1,0:T(8,128)(2,1)S(1)} %fusion.3), channel_id=1, replica_groups=mesh['span'=4,'heads'=8] {'span'}, dimensions={0} | all-to-all | bytes 1572864 | tf_op jit(solution)/shard_map/all_to_all | solution.py:27
  26.5 0.0 all-gather.4.cloned.1.call-update
  26.5 3.3 %all-to-all-start.1 = ((bf16[4,192,64]{1,2,0:T(8,128)(2,1)}), bf16[4,192,64]{1,2,0:T(8,128)(2,1)S(1)}, u32[]{:S(2)}, u32[]{:S(2)}) async-start(bf16[4,192,64]{1,2,0:T(8,128)(2,1)} %param.6), calls=%async_computation.1 | async-start | bytes 262144 | tf_op jit(solution)/shard_map/all_to_all | solution.py:28
  29.9 0.0 copy-done.2
  29.9 0.2 copy.19
  30.1 4.8 %all-to-all-done.1 = bf16[4,192,64]{1,2,0:T(8,128)(2,1)S(1)} async-done(((bf16[4,192,64]{1,2,0:T(8,128)(2,1)}), bf16[4,192,64]{1,2,0:T(8,128)(2,1)S(1)}, u32[]{:S(2)}, u32[]{:S(2)}) %all-to-all-start.1) | async-done | bytes 98336 | tf_op jit(solution)/shard_map/all_to_all | solution.py:28
  34.9 0.2 copy.20
  35.0 31.3 %all-gather.1 = bf16[4,1536,64]{2,0,1:T(4,128)(2,1)S(1)} all-gather(bf16[4,192,64]{2,0,1:T(4,128)(2,1)S(1)} %copy.20), channel_id=3, replica_groups=mesh['span'=4,'heads'=8] {'heads'}, dimensions={1}, use_global_device_ids=true | all-gather | bytes 884736 | tf_op jit(solution)/shard_map/all_gather | solution.py:38
  66.4 1.2 copy.21
  67.5 0.1 copy.24
  67.7 35.9 %all-gather.4.cloned.1.call-done = bf16[4,1536,512]{2,1,0:T(8,128)(2,1)} async-done(((bf16[4,192,512]{2,1,0:T(8,128)(2,1)}), bf16[4,1536,512]{2,1,0:T(8,128)(2,1)}) %all-gather.4.cloned.1.call-update) | async-done | bytes 6291472 | tf_op jit(solution)/shard_map/all_gather | solution.py:37
  103.6 4.6 %fusion.5 = f32[6144,256]{0,1:S(1)} fusion(bf16[6144,512]{1,0:T(8,128)(2,1)} %bitcast.17, bf16[512,256]{0,1:T(8,128)(2,1)S(1)} %bitcast.21), kind=kOutput, calls=%fused_computation.11 | convolution fusion | flops 1610612736 | bytes 12845056
  108.2 0.0 copy-start.1
  108.2 0.4 convert_bitcast_fusion
  108.6 0.0 copy-done
  108.6 2.3 %copy-done.1 = bf16[4,1536,512]{2,1,0:T(8,128)(2,1)S(1)} copy-done((bf16[4,1536,512]{2,1,0:T(8,128)(2,1)S(1)}, bf16[4,1536,512]{2,1,0:T(8,128)(2,1)}, u32[]{:S(2)}) %copy-start.1) | copy-done | bytes 6291480
  111.0 1.8 %fusion = bf16[1,6144,2,128]{3,1,2,0:T(8,128)(2,1)S(1)} fusion(bf16[6144,512,1]{1,0,2:T(8,128)(2,1)S(1)} %bitcast.18, bf16[512,2,128]{2,1,0:T(2,128)(2,1)S(1)} %copy-done), kind=kOutput, calls=%fused_computation.1 | convolution fusion | flops 1612185600 | bytes 9699328 | tf_op jit(solution)/shard_map/btr,rhk->bthk/dot_general | solution.py:12
  112.8 26.8 %copy.23 = bf16[1,6144,2,128]{3,2,1,0:T(2,128)(2,1)} copy(bf16[1,6144,2,128]{3,1,2,0:T(8,128)(2,1)S(1)} %fusion) | data formatting | bytes 6291456
  139.5 0.1 broadcast_in_dim.10
  139.7 2.5 %pad_maximum_fusion = bf16[1,6144,2,192]{1,3,2,0:T(8,128)(2,1)} fusion(bf16[1,6144,2,64]{1,3,2,0:T(8,128)(2,1)S(1)} %broadcast_in_dim.10, bf16[1,6144,2,128]{1,3,2,0:T(8,128)(2,1)S(1)} %convert_bitcast_fusion), kind=kLoop, calls=%fused_computation.2 | loop fusion | flops 9437184 | bytes 9437184 | tf_op jit(solution)/shard_map/concatenate | solution.py:15
  (1 shorter events, 0.0 us)
Async XLA Ops:
  7.2 101.5 %copy-start = (bf16[512,2,128]{2,1,0:T(2,128)(2,1)S(1)}, bf16[512,2,128]{2,1,0:T(2,128)(2,1)}, u32[]{:S(2)}) copy-start(bf16[512,2,128]{2,1,0:T(2,128)(2,1)} %param.9) | copy-start | bytes 786436
  7.2 22.7 %copy-start.2 = (bf16[512,2,128]{2,1,0:T(2,128)(2,1)S(1)}, bf16[512,2,128]{2,1,0:T(2,128)(2,1)}, u32[]{:S(2)}) copy-start(bf16[512,2,128]{2,1,0:T(2,128)(2,1)} %param.8) | copy-start | bytes 786436
  7.2 96.4 %all-gather.4.cloned.1.call-start = ((), (), s32[]{:S(2)}) async-start(), calls=%async_computation.2 | async-start | bytes 7077888 | tf_op jit(solution)/shard_map/all_gather | solution.py:37
  26.5 8.3 %all-to-all-start.1 = ((bf16[4,192,64]{1,2,0:T(8,128)(2,1)}), bf16[4,192,64]{1,2,0:T(8,128)(2,1)S(1)}, u32[]{:S(2)}, u32[]{:S(2)}) async-start(bf16[4,192,64]{1,2,0:T(8,128)(2,1)} %param.6), calls=%async_computation.1 | async-start | bytes 262144 | tf_op jit(solution)/shard_map/all_to_all | solution.py:28
  108.2 2.8 %copy-start.1 = (bf16[4,1536,512]{2,1,0:T(8,128)(2,1)S(1)}, bf16[4,1536,512]{2,1,0:T(8,128)(2,1)}, u32[]{:S(2)}) copy-start(bf16[4,1536,512]{2,1,0:T(8,128)(2,1)} %all-gather.4.cloned.1.call-done) | copy-start | bytes 18874372
Sparse Core Ops, SparseCore 0:
  26.6 76.8 all-gather.3
where the time goes:
time: 149 us
  blocking collectives  47.8 us (32%)
  waiting for transfers between devices  40.7 us (27%)
  local copies, waits for them, and re-layouts  30.9 us (21%)
  between operations  14.2 us (10%)
  matrix products  6.4 us (4%)
  other arithmetic  5.74 us (4%)
  starting transfers between devices  3.38 us (2%)
    all_gather x1, waiting for transfers between devices, per_device(): lax.all_gather(rows_cut, 'heads', axis=2, tiled=True)  35.9 us
    all_gather x1, blocking collectives, per_device(): lax.all_gather(rotary_cut, 'heads', axis=2, tiled=True)  31.3 us
    unnamed x9, local copies, waits for them, and re-layouts  29.4 us
    all_to_all x1, blocking collectives, per_device(): lax.all_to_all(rows_ready, 'span', split_axis=0, concat_axis=1, tiled=True)  16.4 us
    all_to_all x1, waiting for transfers between devices, per_device(): lax.all_to_all(rotary_rows, 'span', split_axis=0, concat_axis=1, tiled=True)  4.81 us
    unnamed x1, matrix products  4.61 us
    all_to_all x1, starting transfers between devices, per_device(): lax.all_to_all(rotary_rows, 'span', split_axis=0, concat_axis=1, tiled=True)  3.34 us
  transfers between devices with their start and end apart: 2, of which 2 were waited for; matrix products, arithmetic and copies ran while one was open for 1% of the time, Pallas kernels for 0%

commit v1 on v0

--- a/solution.py
+++ b/solution.py
@@ -24,7 +24,12 @@
 def per_device(latents, rotary_rows, latent_gain, key_up, value_up):
     rows_ready = root_norm(latents.astype(jnp.float32), latent_gain).astype(jnp.bfloat16)
     rows_moved, rotary_moved = (
-        lax.all_to_all(rows_ready, "span", split_axis=0, concat_axis=1, tiled=True),
+        jnp.concatenate(
+            lax.all_to_all(
+                jnp.stack(jnp.split(rows_ready, lax.axis_size("span"), axis=0)), "span", 0, 0
+            ),
+            axis=1,
+        ),
         lax.all_to_all(rotary_rows, "span", split_axis=0, concat_axis=1, tiled=True),
     )
     rows_cut = rows_moved.reshape(

time: 149 us -> 150 us (level)
  no operation moved by 1% of the time
where the time goes in v1:
time: 150 us; the launch traced here: 149 us
  blocking collectives  47.8 us (32%)
  waiting for transfers between devices  40.7 us (27%)
  local copies, waits for them, and re-layouts  31 us (21%)
  between operations  14.2 us (9%)
  matrix products  6.41 us (4%)
  other arithmetic  5.84 us (4%)
  starting transfers between devices  3.38 us (2%)
    all_gather x1, waiting for transfers between devices, per_device(): lax.all_gather(rows_cut, 'heads', axis=2, tiled=True)  35.9 us
    all_gather x1, blocking collectives, per_device(): lax.all_gather(rotary_cut, 'heads', axis=2, tiled=True)  31.3 us
    unnamed x9, local copies, waits for them, and re-layouts  29.4 us
    all_to_all x1, blocking collectives, per_device(): lax.all_to_all(jnp.stack(jnp.split(rows_ready, lax.axis_size('span'), axi...  16.4 us
    all_to_all x1, waiting for transfers between devices, per_device(): lax.all_to_all(rotary_rows, 'span', split_axis=0, concat_axis=1, tiled=True)  4.81 us
    unnamed x1, matrix products  4.61 us
    all_to_all x1, starting transfers between devices, per_device(): lax.all_to_all(rotary_rows, 'span', split_axis=0, concat_axis=1, tiled=True)  3.34 us
  transfers between devices with their start and end apart: 2, of which 2 were waited for; matrix products, arithmetic and copies ran while one was open for 1% of the time, Pallas kernels for 0%

profile of v1, /device:TPU:0, one launch (start us, length us, event | category | flops | bytes accessed | tf_op | source)
XLA Modules:
  0.0 149.2 jit_solution(4396283261866898691)
XLA Ops:
  7.2 0.0 copy-start
  7.2 0.0 copy-start.2
  7.2 0.0 all-gather.4.cloned.1.call-start
  7.2 1.4 fusion.1
  8.7 1.4 fusion.3
  10.1 0.1 slice_bitcast_fusion.3
  10.1 0.1 pad_maximum_fusion.1
  10.2 16.4 %all_to_all.14 = bf16[4,1,192,512]{3,2,1,0:T(8,128)(2,1)} all-to-all(bf16[4,1,192,512]{3,2,1,0:T(8,128)(2,1)S(1)} %pad_maximum_fusion.1), channel_id=1, replica_groups=mesh['span'=4,'heads'=8] {'span'}, dimensions={0} | all-to-all | bytes 1572864 | tf_op jit(solution)/shard_map/all_to_all | solution.py:28
  26.7 0.0 all-gather.4.cloned.1.call-update
  26.7 3.3 %all-to-all-start.1 = ((bf16[4,192,64]{1,2,0:T(8,128)(2,1)}), bf16[4,192,64]{1,2,0:T(8,128)(2,1)S(1)}, u32[]{:S(2)}, u32[]{:S(2)}) async-start(bf16[4,192,64]{1,2,0:T(8,128)(2,1)} %param.6), calls=%async_computation.1 | async-start | bytes 262144 | tf_op jit(solution)/shard_map/all_to_all | solution.py:33
  30.0 0.0 copy-done.2
  30.1 0.2 copy.19
  30.2 4.8 %all-to-all-done.1 = bf16[4,192,64]{1,2,0:T(8,128)(2,1)S(1)} async-done(((bf16[4,192,64]{1,2,0:T(8,128)(2,1)}), bf16[4,192,64]{1,2,0:T(8,128)(2,1)S(1)}, u32[]{:S(2)}, u32[]{:S(2)}) %all-to-all-start.1) | async-done | bytes 98336 | tf_op jit(solution)/shard_map/all_to_all | solution.py:33
  35.0 0.2 copy.20
  35.2 31.3 %all-gather.1 = bf16[4,1536,64]{2,0,1:T(4,128)(2,1)S(1)} all-gather(bf16[4,192,64]{2,0,1:T(4,128)(2,1)S(1)} %copy.20), channel_id=3, replica_groups=mesh['span'=4,'heads'=8] {'heads'}, dimensions={1}, use_global_device_ids=true | all-gather | bytes 884736 | tf_op jit(solution)/shard_map/all_gather | solution.py:43
  66.6 1.2 copy.21
  67.7 0.1 copy.24
  67.9 35.9 %all-gather.4.cloned.1.call-done = bf16[4,1,1536,512]{3,2,1,0:T(8,128)(2,1)} async-done(((bf16[4,1,192,512]{3,2,1,0:T(8,128)(2,1)}), bf16[4,1,1536,512]{3,2,1,0:T(8,128)(2,1)}) %all-gather.4.cloned.1.call-update) | async-done | bytes 6291472 | tf_op jit(solution)/shard_map/all_gather | solution.py:42
  103.7 4.6 %fusion.5 = f32[6144,256]{0,1:S(1)} fusion(bf16[6144,512]{1,0:T(8,128)(2,1)} %bitcast.25, bf16[512,256]{0,1:T(8,128)(2,1)S(1)} %bitcast.29), kind=kOutput, calls=%fused_computation.16 | convolution fusion | flops 1610612736 | bytes 12845056
  108.4 0.0 copy-start.1
  108.4 0.4 convert_bitcast_fusion
  108.8 0.0 copy-done
  108.8 2.3 %copy-done.1 = bf16[4,1,1536,512]{3,2,1,0:T(8,128)(2,1)S(1)} copy-done((bf16[4,1,1536,512]{3,2,1,0:T(8,128)(2,1)S(1)}, bf16[4,1,1536,512]{3,2,1,0:T(8,128)(2,1)}, u32[]{:S(2)}) %copy-start.1) | copy-done | bytes 6291480
  111.1 1.8 %fusion = bf16[1,6144,2,128]{3,1,2,0:T(8,128)(2,1)S(1)} fusion(bf16[6144,512,1]{1,0,2:T(8,128)(2,1)S(1)} %bitcast.26, bf16[512,2,128]{2,1,0:T(2,128)(2,1)S(1)} %copy-done), kind=kOutput, calls=%fused_computation.1 | convolution fusion | flops 1612185600 | bytes 9699328 | tf_op jit(solution)/shard_map/btr,rhk->bthk/dot_general | solution.py:12
  112.9 26.8 %copy.23 = bf16[1,6144,2,128]{3,2,1,0:T(2,128)(2,1)} copy(bf16[1,6144,2,128]{3,1,2,0:T(8,128)(2,1)S(1)} %fusion) | data formatting | bytes 6291456
  139.7 0.1 broadcast_in_dim.10
  139.9 2.5 %pad_maximum_fusion = bf16[1,6144,2,192]{1,3,2,0:T(8,128)(2,1)} fusion(bf16[1,6144,2,64]{1,3,2,0:T(8,128)(2,1)S(1)} %broadcast_in_dim.10, bf16[1,6144,2,128]{1,3,2,0:T(8,128)(2,1)S(1)} %convert_bitcast_fusion), kind=kLoop, calls=%fused_computation.2 | loop fusion | flops 9437184 | bytes 9437184 | tf_op jit(solution)/shard_map/concatenate | solution.py:15
  (1 shorter events, 0.0 us)
Async XLA Ops:
  7.2 101.6 %copy-start = (bf16[512,2,128]{2,1,0:T(2,128)(2,1)S(1)}, bf16[512,2,128]{2,1,0:T(2,128)(2,1)}, u32[]{:S(2)}) copy-start(bf16[512,2,128]{2,1,0:T(2,128)(2,1)} %param.9) | copy-start | bytes 786436
  7.2 22.9 %copy-start.2 = (bf16[512,2,128]{2,1,0:T(2,128)(2,1)S(1)}, bf16[512,2,128]{2,1,0:T(2,128)(2,1)}, u32[]{:S(2)}) copy-start(bf16[512,2,128]{2,1,0:T(2,128)(2,1)} %param.8) | copy-start | bytes 786436
  7.2 96.6 %all-gather.4.cloned.1.call-start = ((), (), s32[]{:S(2)}) async-start(), calls=%async_computation.2 | async-start | bytes 7077888 | tf_op jit(solution)/shard_map/all_gather | solution.py:42
  26.7 8.3 %all-to-all-start.1 = ((bf16[4,192,64]{1,2,0:T(8,128)(2,1)}), bf16[4,192,64]{1,2,0:T(8,128)(2,1)S(1)}, u32[]{:S(2)}, u32[]{:S(2)}) async-start(bf16[4,192,64]{1,2,0:T(8,128)(2,1)} %param.6), calls=%async_computation.1 | async-start | bytes 262144 | tf_op jit(solution)/shard_map/all_to_all | solution.py:33
  108.4 2.8 %copy-start.1 = (bf16[4,1,1536,512]{3,2,1,0:T(8,128)(2,1)S(1)}, bf16[4,1,1536,512]{3,2,1,0:T(8,128)(2,1)}, u32[]{:S(2)}) copy-start(bf16[4,1,1536,512]{3,2,1,0:T(8,128)(2,1)} %all-gather.4.cloned.1.call-done) | copy-start | bytes 18874372
Sparse Core Ops, SparseCore 0:
  26.8 76.8 all-gather.3
